TPU v7x, 256 devices: a whole 4x4x8 slice. The times are simulated.
256 devices in a mesh: row: 128 (over y, x, z), col: 2 (over core).
Axes of the slice: x: 4, y: 4, z: 8, core: 2. Of those that a mesh axis runs over, the one named last changes fastest.
Arguments:
- features: float32 [64, 32768], P(None, ('row', 'col')), may hold values from -12 to 12
- initial: float32 [32768], P(('row', 'col')), may hold values from 0.1 to 90, as said below
Outputs:
- dist: float32 [32768], P(('row', 'col'))
- residuals: float32 [2], replicated
Inputs may be any that keep to these rules, and one draw needn't show every extreme that they name: `initial`: positive starting weights of the policies.
All inputs are finite; a program needn't handle non-finite values.
Results may differ from a plain program's by a relative error of at most 0.0003.
Values sent between devices are 32-bit elements; how exact they have to be, the bound alone decides.
No kernel may reach another device: no remote copies, remote signals or barrier semaphores. Data moves between devices by JAX's collectives and lax.ppermute only.
A program may use at most 64 MiB of HBM per device.

v0:
```python
import functools
import math

import jax
import jax.numpy as jnp
from jax import lax
from jax.sharding import Mesh
from jax.sharding import PartitionSpec as P

NPOL = 32768
ITERS = 2
ROW_COL = ("row_0", "row_1", "row_2", "col")
ROW = ("row_0", "row_1", "row_2")


intensity = 0.25
column_block = 2048


def in_order(blocks, dim):
    lengths = list(blocks.shape[1:])
    lengths[dim] *= blocks.shape[0]
    return jnp.moveaxis(blocks, 0, dim).reshape(lengths)


def copy_for_each(array, axis):
    copies = jnp.broadcast_to(array, (lax.axis_size(axis), *array.shape))
    return lax.all_to_all(copies, axis, split_axis=0, concat_axis=0, tiled=True)


def gathered_copies(array, axis, dim):
    return in_order(copy_for_each(array, axis), dim)


def one_axis_at_a_time(array, axes):
    return functools.reduce(lax.psum, axes, array)


def all_blocks(array, axes, turns):
    blocks = array[None]
    for k in turns:
        blocks = lax.all_gather(blocks, axes[k], axis=0, tiled=True)
    block = [lax.axis_size(axes[k]) for k in reversed(turns)]
    blocks = blocks.reshape(*block, *array.shape)
    turned = sorted(range(len(turns)), key=lambda place: turns[len(turns) - 1 - place])
    return blocks.transpose(*turned, *range(len(turns), blocks.ndim)).reshape(-1, *array.shape)


def gathered_by_axis(array, axes, turns, dim):
    return in_order(all_blocks(array, axes, turns), dim)


def cut_along(array, dim, count):
    lengths = array.shape
    blocks = array.reshape(*lengths[:dim], count, lengths[dim] // count, *lengths[dim + 1 :])
    return jnp.moveaxis(blocks, dim, 0)


def sum_at_owner(array, axis, dim):
    blocks = cut_along(array, dim, lax.axis_size(axis))
    arrived = lax.all_to_all(blocks, axis, split_axis=0, concat_axis=0, tiled=True)
    return arrived.sum(axis=0)


def sum_in_two_steps(array, axes, dim):
    far, near = axes
    blocks = cut_along(array, dim, lax.axis_size(far))
    nearer = sum_at_owner(blocks, near, dim + 1)
    arrived = lax.all_to_all(nearer, far, split_axis=0, concat_axis=0, tiled=True)
    return arrived.sum(axis=0)


def of_everyone(array, axis):
    everything = copy_for_each(array, axis)
    return jnp.sum(everything, axis=0)


def by_axis(array, axes):
    far, near = axes
    nearer = of_everyone(array, near)
    return of_everyone(nearer, far)


def in_one(arrays, axis):
    line, at, done = (jnp.concatenate([a.reshape(-1) for a in arrays]), 0, [])
    total = by_axis(line, axis)
    for a in arrays:
        done.append(total[at : at + a.size].reshape(a.shape))
        at += a.size
    return tuple(done)


def column_pass(row_side, rows_mass, column_feats):
    columns = column_feats.shape[1]
    block_width = math.gcd(columns, column_block)
    count_blocks = columns // block_width

    def one_block(block_index):
        segment = lax.dynamic_slice_in_dim(column_feats, block_index * block_width, block_width, 1)
        payoff = jnp.einsum("kr,kc->rc", row_side, segment, precision=lax.Precision.HIGHEST)
        moves = jax.nn.sigmoid(intensity * payoff)
        inflow = jnp.dot(rows_mass, moves, precision=lax.Precision.HIGHEST)
        return (inflow, jnp.sum(moves, axis=1))

    inflows, totals = lax.map(one_block, jnp.arange(count_blocks, dtype=jnp.int32))
    return (inflows.reshape(columns), jnp.sum(totals, axis=0))


def on_device(features, initial):
    half_feat = features.shape[0] // 2
    row_feats = gathered_copies(features, "col", 1)
    row_side = jnp.concatenate([row_feats[half_feat:], -row_feats[:half_feat]], axis=0)
    step_rate = 1.0 / NPOL
    weights = initial / one_axis_at_a_time(jnp.sum(initial), ROW_COL)
    column_feats = gathered_by_axis(features, ROW, (0, 1, 2), 1)
    changes = []
    pending = jnp.zeros((), jnp.float32)
    own_totals = jnp.zeros_like(weights)
    for iteration in range(ITERS):
        rows_mass = gathered_copies(weights, "col", 0)
        inflow, totals = column_pass(row_side, rows_mass, column_feats)
        if iteration == 0:
            own_totals = sum_at_owner(totals, "col", 0)
        summed = sum_in_two_steps(inflow, ("row_0", ("row_1", "row_2")), 0)
        advanced = step_rate * summed + weights * (1.0 - step_rate * own_totals)
        normalizer, earlier = in_one(
            (jnp.sum(advanced), pending), ("row_0", ("row_1", "row_2", "col"))
        )
        if iteration > 0:
            changes.append(earlier)
        updated = advanced / normalizer
        pending = jnp.sum(jnp.abs(updated - weights))
        weights = updated
    changes.append(one_axis_at_a_time(pending, ROW_COL))
    return (NPOL * weights, jnp.stack(changes))


def solution(mesh):
    torus = Mesh(
        mesh.devices.reshape(4, 4, 8, mesh.shape["col"]), ("row_0", "row_1", "row_2", "col")
    )
    in_specs = (P(None, ROW_COL), P(ROW_COL))
    out_specs = (P(ROW_COL), P())
    return jax.shard_map(
        on_device, mesh=torus, in_specs=in_specs, out_specs=out_specs, check_vma=False
    )
```

profile of v0, /device:TPU:1, one launch (start us, length us, event | category | flops | bytes accessed | tf_op | source)
XLA Modules:
  0.0 353.5 jit_solution(2726497459547294447)
XLA Ops:
  7.2 10.8 %all-gather = f32[256,128]{1,0:T(8,128)S(1)} all-gather(f32[64,128]{1,0:T(8,128)} %param.6), channel_id=2, replica_groups=mesh['row_0'=4,'row_1'=4,'row_2'=8,'col'=2] {'row_0'}, dimensions={0}, use_global_device_ids=true | all-gather | bytes 163840 | tf_op jit(solution)/shard_map/all_gather | solution.py:42
  18.0 11.0 %all_gather.10 = f32[16,64,128]{2,1,0:T(8,128)} all-gather(f32[4,64,128]{2,1,0:T(8,128)S(1)} %bitcast.79), channel_id=1, replica_groups=mesh['row_0'=4,'row_1'=4,'row_2'=8,'col'=2] {'row_1'}, dimensions={0}, use_global_device_ids=true | all-gather | bytes 655360 | tf_op jit(solution)/shard_map/all_gather | solution.py:42
  30.3 8.7 %psum.56 = f32[]{:T(128)} all-reduce(f32[]{:T(128)} %reduce_sum.144), channel_id=1, replica_groups=mesh['row_0'=4,'row_1'=4,'row_2'=8,'col'=2] {'row_0'}, use_global_device_ids=true, to_apply=%region_1.0 | all-reduce | flops 1 | bytes 8 | tf_op jit(solution)/shard_map/psum | solution.py:36
  39.0 9.2 %psum.57 = f32[]{:T(128)} all-reduce(f32[]{:T(128)} %psum.56), channel_id=1, replica_groups=mesh['row_0'=4,'row_1'=4,'row_2'=8,'col'=2] {'row_1'}, use_global_device_ids=true, to_apply=%region_2.0 | all-reduce | flops 1 | bytes 8 | tf_op jit(solution)/shard_map/psum | solution.py:36
  48.2 19.2 %psum.58 = f32[]{:T(128)} all-reduce(f32[]{:T(128)} %psum.57), channel_id=1, replica_groups=mesh['row_0'=4,'row_1'=4,'row_2'=8,'col'=2] {'row_2'}, use_global_device_ids=true, to_apply=%region_3.0 | all-reduce | flops 1 | bytes 8 | tf_op jit(solution)/shard_map/psum | solution.py:36
  67.4 1.4 broadcast_in_dim.39
  68.8 15.1 %all-to-all-start = ((f32[2,64,128]{2,1,0:T(8,128)}), f32[2,64,128]{2,1,0:T(8,128)S(1)}, u32[]{:S(2)}, u32[]{:S(2)}) async-start(f32[2,64,128]{2,1,0:T(8,128)} %broadcast_in_dim.39), calls=%async_computation | async-start | bytes 131072 | tf_op jit(solution)/shard_map/all_to_all | solution.py:28
  83.9 3.1 psum.59
  88.9 3.3 all-to-all-start.1
  92.2 2.5 copy.21
  94.7 2.2 copy.45
  96.9 52.0 %while.22 = (s32[]{:T(128)}, f32[8,2048]{1,0:T(8,128)S(1)}, f32[8,256]{1,0:T(8,128)S(1)}, s32[8]{0:T(128)S(1)}, f32[64,16384]{1,0:T(8,128)}, /*index=5*/f32[64,2...) while((s32[]{:T(128)}, f32[8,2048]{1,0:T(8,128)S(1)}, ...), condition=%wide.region_7.8_spmd, body=%wide.region_5.7_spmd.sunk | while | flops 411565824 | bytes 4812979 | solution.py:105
  98.1 3.2 fusion.40
  101.3 1.9 fusion.41
  104.6 3.2 fusion.40
  107.8 1.9 fusion.41
  111.1 3.2 fusion.40
  114.3 1.9 fusion.41
  117.6 3.2 fusion.40
  120.8 1.9 fusion.41
  124.1 3.2 fusion.40
  127.3 1.9 fusion.41
  130.6 3.2 fusion.40
  133.8 1.9 fusion.41
  137.1 3.2 fusion.40
  140.3 1.9 fusion.41
  143.6 3.2 fusion.40
  146.8 1.9 fusion.41
  149.6 6.0 %all-to-all-start.2 = ((f32[32,4,128]{2,1,0:T(4,128)}), f32[32,4,128]{2,1,0:T(4,128)S(1)}, u32[]{:S(2)}, u32[]{:S(2)}) async-start(f32[32,4,128]{2,1,0:T(4,128)} %copy.25), calls=%async_computation.2 | async-start | bytes 131072 | tf_op jit(solution)/shard_map/all_to_all | solution.py:61
  156.2 8.3 %all-to-all-done.2 = f32[32,4,128]{2,1,0:T(4,128)S(1)} async-done(((f32[32,4,128]{2,1,0:T(4,128)}), f32[32,4,128]{2,1,0:T(4,128)S(1)}, u32[]{:S(2)}, u32[]{:S(2)}) %all-to-all-start.2) | async-done | bytes 65568 | tf_op jit(solution)/shard_map/all_to_all | solution.py:61
  164.5 5.4 %all-to-all-start.4 = ((f32[2,1,128]{2,1,0:T(1,128)}), f32[2,1,128]{2,1,0:T(1,128)S(1)}, u32[]{:S(2)}, u32[]{:S(2)}) async-start(f32[2,1,128]{2,1,0:T(1,128)} %bitcast.18), calls=%async_computation.4 | async-start | bytes 2048 | tf_op jit(solution)/shard_map/all_to_all | solution.py:61
  170.9 4.0 %all-to-all-start.3 = ((f32[4,1,128]{2,1,0:T(1,128)}), f32[4,1,128]{2,1,0:T(1,128)S(1)}, u32[]{:S(2)}, u32[]{:S(2)}) async-start(f32[4,1,128]{2,1,0:T(1,128)} %bitcast.17), calls=%async_computation.3 | async-start | bytes 4096 | tf_op jit(solution)/shard_map/all_to_all | solution.py:69
  174.9 4.0 %all-to-all-done.3 = f32[4,1,128]{2,1,0:T(1,128)S(1)} async-done(((f32[4,1,128]{2,1,0:T(1,128)}), f32[4,1,128]{2,1,0:T(1,128)S(1)}, u32[]{:S(2)}, u32[]{:S(2)}) %all-to-all-start.3) | async-done | bytes 2080 | tf_op jit(solution)/shard_map/all_to_all | solution.py:69
  181.5 5.9 %all-to-all-start.5 = ((f32[64,1,2]{2,1,0:T(1,128)}), f32[64,1,2]{2,1,0:T(1,128)S(1)}, u32[]{:S(2)}, u32[]{:S(2)}) async-start(f32[64,1,2]{2,1,0:T(1,128)} %broadcast_in_dim.42), calls=%async_computation.5 | async-start | bytes 65536 | tf_op jit(solution)/shard_map/all_to_all | solution.py:28
  187.4 9.4 %all-to-all-done.5 = f32[64,1,2]{2,1,0:T(1,128)S(1)} async-done(((f32[64,1,2]{2,1,0:T(1,128)}), f32[64,1,2]{2,1,0:T(1,128)S(1)}, u32[]{:S(2)}, u32[]{:S(2)}) %all-to-all-start.5) | async-done | bytes 544 | tf_op jit(solution)/shard_map/all_to_all | solution.py:28
  196.9 6.5 %all_to_all.78 = f32[4,1,2]{2,1,0:T(1,128)S(1)} all-to-all(f32[4,1,2]{2,1,0:T(1,128)S(1)} %broadcast_in_dim.43), channel_id=1, replica_groups=mesh['row_0'=4,'row_1'=4,'row_2'=8,'col'=2] {'row_0'}, dimensions={0} | all-to-all | bytes 64 | tf_op jit(solution)/shard_map/all_to_all | solution.py:28
  204.7 5.2 %all_to_all.79 = f32[2,1,128]{2,1,0:T(1,128)S(1)} all-to-all(f32[2,1,128]{2,1,0:T(1,128)S(1)} %broadcast_in_dim.44), channel_id=1, replica_groups=mesh['row_0'=4,'row_1'=4,'row_2'=8,'col'=2] {'col'}, dimensions={0} | all-to-all | bytes 2048 | tf_op jit(solution)/shard_map/all_to_all | solution.py:28
  209.9 51.2 %while.23 = (s32[]{:T(128)}, f32[8,2048]{1,0:T(8,128)S(1)}, s32[8]{0:T(128)S(1)}, f32[64,16384]{1,0:T(8,128)}, f32[64,256]{1,0:T(8,128)S(1)}, /*index=5*/f32[256...) while((s32[]{:T(128)}, f32[8,2048]{1,0:T(8,128)S(1)}, s32[8]{0:T(128)S(1)}, ...), condition=%wide.region_16.17_spmd, body=%wide.region_15.16_spmd.sunk | while | flops 411041792 | bytes 4809895 | solution.py:105
  211.1 3.1 fusion.46
  214.2 1.9 fusion.47
  217.5 3.1 fusion.46
  220.6 1.9 fusion.47
  223.9 3.1 fusion.46
  227.0 1.9 fusion.47
  230.3 3.1 fusion.46
  233.4 1.9 fusion.47
  236.7 3.1 fusion.46
  239.8 1.9 fusion.47
  243.2 3.1 fusion.46
  246.3 1.9 fusion.47
  249.6 3.1 fusion.46
  252.7 1.9 fusion.47
  256.0 3.1 fusion.46
  259.1 1.9 fusion.47
  261.2 11.8 %all_to_all.81 = f32[32,4,128]{2,1,0:T(4,128)S(1)} all-to-all(f32[32,4,128]{2,1,0:T(4,128)S(1)} %copy.29), channel_id=1, replica_groups=mesh['row_0'=4,'row_1'=4,'row_2'=8,'col'=2] {'row_1','row_2'}, dimensions={0} | all-to-all | bytes 131072 | tf_op jit(solution)/shard_map/all_to_all | solution.py:61
  273.1 6.5 %all_to_all.82 = f32[4,1,128]{2,1,0:T(1,128)S(1)} all-to-all(f32[4,1,128]{2,1,0:T(1,128)S(1)} %bitcast.88), channel_id=1, replica_groups=mesh['row_0'=4,'row_1'=4,'row_2'=8,'col'=2] {'row_0'}, dimensions={0} | all-to-all | bytes 4096 | tf_op jit(solution)/shard_map/all_to_all | solution.py:69
  280.2 1.4 pad_maximum_fusion.1
  281.6 15.4 %all_to_all.83 = f32[64,1,2]{2,1,0:T(1,128)S(1)} all-to-all(f32[64,1,2]{2,1,0:T(1,128)S(1)} %broadcast_in_dim.45), channel_id=1, replica_groups=mesh['row_0'=4,'row_1'=4,'row_2'=8,'col'=2] {'row_1','row_2','col'}, dimensions={0} | all-to-all | bytes 1024 | tf_op jit(solution)/shard_map/all_to_all | solution.py:28
  297.0 6.5 %all_to_all.80 = f32[4,1,2]{2,1,0:T(1,128)S(1)} all-to-all(f32[4,1,2]{2,1,0:T(1,128)S(1)} %broadcast_in_dim.46), channel_id=1, replica_groups=mesh['row_0'=4,'row_1'=4,'row_2'=8,'col'=2] {'row_0'}, dimensions={0} | all-to-all | bytes 64 | tf_op jit(solution)/shard_map/all_to_all | solution.py:28
  305.4 7.5 %psum.60 = f32[]{:T(128)} all-reduce(f32[]{:T(128)} %get-tuple-element.101), channel_id=1, replica_groups=mesh['row_0'=4,'row_1'=4,'row_2'=8,'col'=2] {'row_0'}, use_global_device_ids=true, to_apply=%region_24.25 | all-reduce | flops 1 | bytes 8 | tf_op jit(solution)/shard_map/psum | solution.py:36
  312.9 7.4 %psum.61 = f32[]{:T(128)} all-reduce(f32[]{:T(128)} %psum.60), channel_id=1, replica_groups=mesh['row_0'=4,'row_1'=4,'row_2'=8,'col'=2] {'row_1'}, use_global_device_ids=true, to_apply=%region_25.26 | all-reduce | flops 1 | bytes 8 | tf_op jit(solution)/shard_map/psum | solution.py:36
  320.3 11.6 %psum.62 = f32[]{:T(128)} all-reduce(f32[]{:T(128)} %psum.61), channel_id=1, replica_groups=mesh['row_0'=4,'row_1'=4,'row_2'=8,'col'=2] {'row_2'}, use_global_device_ids=true, to_apply=%region_26.27 | all-reduce | flops 1 | bytes 8 | tf_op jit(solution)/shard_map/psum | solution.py:36
  331.9 12.3 %psum.63 = f32[1]{0:T(128)} all-reduce(f32[1]{0:T(128)} %bitcast.28), channel_id=1, replica_groups=mesh['row_0'=4,'row_1'=4,'row_2'=8,'col'=2] {'col'}, use_global_device_ids=true, to_apply=%region_27.28 | all-reduce | flops 1 | bytes 8 | tf_op jit(solution)/shard_map/psum | solution.py:36
  344.8 1.8 pad_maximum_fusion.2
  (85 shorter events, 25.7 us)
Async XLA Ops:
  7.2 85.0 %all-gather.3.cloned.1.call-start = ((), (), s32[]{:S(2)}) async-start(), calls=%async_computation.12 | async-start | bytes 4718592 | tf_op jit(solution)/shard_map/all_gather | solution.py:42
  68.8 19.5 %all-to-all-start = ((f32[2,64,128]{2,1,0:T(8,128)}), f32[2,64,128]{2,1,0:T(8,128)S(1)}, u32[]{:S(2)}, u32[]{:S(2)}) async-start(f32[2,64,128]{2,1,0:T(8,128)} %broadcast_in_dim.39), calls=%async_computation | async-start | bytes 131072 | tf_op jit(solution)/shard_map/all_to_all | solution.py:28
  88.9 8.0 %all-to-all-start.1 = ((f32[2,1,128]{2,1,0:T(1,128)}), f32[2,1,128]{2,1,0:T(1,128)S(1)}, u32[]{:S(2)}, u32[]{:S(2)}) async-start(f32[2,1,128]{2,1,0:T(1,128)} %broadcast_in_dim.41), calls=%async_computation.1 | async-start | bytes 2048 | tf_op jit(solution)/shard_map/all_to_all | solution.py:28
  96.9 82.0 %copy-start = (f32[128]{0:T(128)S(1)}, f32[128]{0:T(128)}, u32[]{:S(2)}) copy-start(f32[128]{0:T(128)} %param.7) | copy-start | bytes 1540
  149.6 14.9 %all-to-all-start.2 = ((f32[32,4,128]{2,1,0:T(4,128)}), f32[32,4,128]{2,1,0:T(4,128)S(1)}, u32[]{:S(2)}, u32[]{:S(2)}) async-start(f32[32,4,128]{2,1,0:T(4,128)} %copy.25), calls=%async_computation.2 | async-start | bytes 131072 | tf_op jit(solution)/shard_map/all_to_all | solution.py:61
  164.5 6.4 %all-to-all-start.4 = ((f32[2,1,128]{2,1,0:T(1,128)}), f32[2,1,128]{2,1,0:T(1,128)S(1)}, u32[]{:S(2)}, u32[]{:S(2)}) async-start(f32[2,1,128]{2,1,0:T(1,128)} %bitcast.18), calls=%async_computation.4 | async-start | bytes 2048 | tf_op jit(solution)/shard_map/all_to_all | solution.py:61
  170.9 8.0 %all-to-all-start.3 = ((f32[4,1,128]{2,1,0:T(1,128)}), f32[4,1,128]{2,1,0:T(1,128)S(1)}, u32[]{:S(2)}, u32[]{:S(2)}) async-start(f32[4,1,128]{2,1,0:T(1,128)} %bitcast.17), calls=%async_computation.3 | async-start | bytes 4096 | tf_op jit(solution)/shard_map/all_to_all | solution.py:69
  181.5 15.3 %all-to-all-start.5 = ((f32[64,1,2]{2,1,0:T(1,128)}), f32[64,1,2]{2,1,0:T(1,128)S(1)}, u32[]{:S(2)}, u32[]{:S(2)}) async-start(f32[64,1,2]{2,1,0:T(1,128)} %broadcast_in_dim.42), calls=%async_computation.5 | async-start | bytes 65536 | tf_op jit(solution)/shard_map/all_to_all | solution.py:28
Sparse Core Ops, SparseCore 0:
  29.2 62.1 all-gather.2
where the time goes:
time: 355 us; the launch traced here: 353 us
  blocking collectives  153 us (43%)
  matrix products  79.7 us (22%)
  starting transfers between devices  39.7 us (11%)
  waiting for transfers between devices  22.1 us (6%)
  local copies, waits for them, and re-layouts  21.5 us (6%)
  between operations  14.1 us (4%)
  other arithmetic  12.9 us (4%)
  loops' own time  10.7 us (3%)
    psum x8, blocking collectives, one_axis_at_a_time(): return functools.reduce(lax.psum, axes, array)  79.1 us
    dot_general x16, matrix products, one_block(): jnp.einsum('kr,kc->rc', row_side, segment, precision=lax.Precision.HIGHEST)  50 us
    all_to_all x4, blocking collectives, copy_for_each(): return lax.all_to_all(copies, axis, split_axis=0, concat_axis=0, tiled=True)  33.5 us
    dot_general x16, matrix products, one_block(): inflow = jnp.dot(rows_mass, moves, precision=lax.Precision.HIGHEST)  29.7 us
    all_to_all x3, starting transfers between devices, copy_for_each(): return lax.all_to_all(copies, axis, split_axis=0, concat_axis=0, tiled=True)  24.3 us
    all_gather x2, blocking collectives, all_blocks(): blocks = lax.all_gather(blocks, axes[k], axis=0, tiled=True)  21.8 us
    all_to_all x1, blocking collectives, sum_at_owner(): lax.all_to_all(blocks, axis, split_axis=0, concat_axis=0, tiled=True)  11.8 us
    all_to_all x2, starting transfers between devices, sum_at_owner(): lax.all_to_all(blocks, axis, split_axis=0, concat_axis=0, tiled=True)  11.4 us
  transfers between devices with their start and end apart: 7, of which 4 were waited for; matrix products, arithmetic and copies ran while one was open for 3% of the time, Pallas kernels for 0%

commit v1 on v0

v1 whole, which is shorter than its diff:
```python
import jax
import jax.numpy as jnp
from jax import lax
from jax.experimental import pallas as pl
from jax.experimental.pallas import tpu as pltpu
from jax.sharding import Mesh
from jax.sharding import PartitionSpec as P

NPOL = 32768
AXES = ("row_0", "row_1", "row_2", "col")
PLANE = ("row_0", "row_1")
LINE = ("row_2", "col")
HALF = 32
FEATS = 64
SLOT = 72
LANES = 128
GROUP = 16
BLOCK = GROUP * LANES
STEP = 1.0 / NPOL
SCALE = 0.125

VMEM = pl.BlockSpec(memory_space=pltpu.VMEM)


def halves(x):
    high = x.astype(jnp.bfloat16).astype(jnp.float32)
    return high, x - high


def first_pass(rows_ref, cols_ref, out_ref, t_ref, lhs, rhs, mass):
    total = jnp.zeros((1, LANES), jnp.float32)
    for g in range(GROUP):
        x = rows_ref[g]
        a, b = x[:HALF] * SCALE, x[HALF:FEATS] * SCALE
        high, low = halves(jnp.concatenate([b, -a], axis=0))
        at = pl.ds(g * LANES, LANES)
        lhs[at, 0:LANES] = jnp.concatenate([high, high], axis=0).T.astype(jnp.bfloat16)
        lhs[at, LANES : 2 * LANES] = jnp.concatenate([low, low], axis=0).T.astype(jnp.bfloat16)
        u = x[FEATS : FEATS + 1]
        total += u
        mass[at, :] = jnp.broadcast_to(u, (LANES, LANES)).T
        high, low = halves(cols_ref[g, :FEATS])
        high, low = high.astype(jnp.bfloat16), low.astype(jnp.bfloat16)
        rhs[:, at] = jnp.concatenate([high, low, high, low], axis=0)
    here = jnp.sum(total)

    width = 2 * LANES
    height = 2 * LANES
    for jt in range(BLOCK // width):
        at = pl.ds(jt * width, width)
        right = rhs[:, at]
        flow = jnp.zeros((8, width), jnp.float32)
        plain = jnp.zeros((8, width), jnp.float32)
        for ic in range(BLOCK // height):
            down = pl.ds(ic * height, height)
            t = jnp.tanh(jnp.dot(lhs[down, :], right, preferred_element_type=jnp.float32))
            t_ref[down, at] = t
            m = mass[down, :]
            weighted = t * jnp.concatenate([m, m], axis=1)
            flow += weighted.reshape(height // 8, 8, width).sum(axis=0)
            plain += t.reshape(height // 8, 8, width).sum(axis=0)
        flow = 0.5 * (here + jnp.sum(flow, axis=0, keepdims=True))
        plain = 0.5 * (BLOCK - jnp.sum(plain, axis=0, keepdims=True))
        for k in range(2):
            lane = slice(k * LANES, (k + 1) * LANES)
            for copy in range(GROUP):
                out_ref[copy, pl.ds(2 * jt + k, 1), :] = flow[:, lane]
                out_ref[copy, pl.ds(GROUP + 2 * jt + k, 1), :] = plain[:, lane]


def second_pass(got_ref, cols_ref, t_ref, out_ref, own_ref, u1_ref, sums):
    both = jnp.sum(got_ref[...], axis=0)
    flow, totals = both[:GROUP], both[GROUP:]
    u0 = cols_ref[:, FEATS, :]
    stay = 1.0 - STEP * totals
    u1 = STEP * flow + u0 * stay
    here = jnp.sum(u1)
    u1_ref[0] = u1
    u1_ref[1] = stay
    u1_ref[2] = u0
    p = lax.axis_index(PLANE)
    for k in range(3):
        own_ref[pl.ds(k, 1), :] = u1_ref[k, pl.ds(p, 1), :]
    across = [jnp.broadcast_to(u1[g : g + 1], (8, LANES)) for g in range(GROUP)]

    def one(n, carry):
        down = pl.ds(pl.multiple_of(n * 8, 8), 8)
        acc = t_ref[down, 0:LANES] * across[0]
        for g in range(1, GROUP):
            acc += t_ref[down, g * LANES : (g + 1) * LANES] * across[g]
        sums[down, :] = acc
        return carry

    lax.fori_loop(0, BLOCK // 8, one, 0, unroll=8)
    for g in range(GROUP):
        turned = sums[g * LANES : (g + 1) * LANES, :].T
        out_ref[g] = 0.5 * (here - jnp.sum(turned, axis=0, keepdims=True))


def advance(got_ref, own_ref, out_ref):
    flow = jnp.sum(got_ref[...], axis=0)
    u1, stay, u0 = own_ref[0:1], own_ref[1:2], own_ref[2:3]
    u2 = STEP * flow + u1 * stay
    three = jnp.concatenate([u2, u1, u0], axis=0)
    many = jnp.concatenate([three] * 8, axis=0)
    for n in range(out_ref.shape[0] // 24):
        out_ref[pl.ds(n * 24, 24), :] = many


def finish(all_ref, mine_ref, dist_ref, change_ref):
    count = all_ref.shape[0] // 3
    u2 = all_ref[pl.ds(0, count, stride=3), :]
    u1 = all_ref[pl.ds(1, count, stride=3), :]
    u0 = all_ref[pl.ds(2, count, stride=3), :]
    n2, n1, n0 = jnp.sum(u2), jnp.sum(u1), jnp.sum(u0)
    w2, w1, w0 = u2 / n2, u1 / n1, u0 / n0
    first = jnp.sum(jnp.abs(w1 - w0))
    second = jnp.sum(jnp.abs(w2 - w1))
    dist_ref[...] = NPOL * (mine_ref[0:1, :] / n2)
    lane = lax.broadcasted_iota(jnp.int32, (1, LANES), 1)
    change_ref[...] = jnp.where(lane == 0, first, second)


def everyone(array, axes):
    return lax.all_to_all(array, axes, split_axis=0, concat_axis=0, tiled=True)


def on_device(features, initial):
    f32 = jnp.float32
    whole = jnp.concatenate([features, initial[None], jnp.zeros((SLOT - FEATS - 1, LANES), f32)], axis=0)
    copies = jnp.broadcast_to(whole, (GROUP, SLOT, LANES))
    cols = everyone(copies, PLANE)
    rows = everyone(copies, LINE)
    out, t = pl.pallas_call(
        first_pass,
        out_shape=(
            jax.ShapeDtypeStruct((GROUP, 2 * GROUP, LANES), f32),
            pltpu.VMEM((BLOCK, BLOCK), f32),
        ),
        in_specs=[VMEM] * 2,
        out_specs=(VMEM, VMEM),
        scratch_shapes=[
            pltpu.VMEM((BLOCK, 2 * LANES), jnp.bfloat16),
            pltpu.VMEM((2 * LANES, BLOCK), jnp.bfloat16),
            pltpu.VMEM((BLOCK, LANES), f32),
        ],
        compiler_params=pltpu.CompilerParams(vmem_limit_bytes=24 << 20),
        name="first_pass",
    )(rows, cols)
    got = everyone(out, PLANE)
    partial, own = pl.pallas_call(
        second_pass,
        out_shape=(
            jax.ShapeDtypeStruct((GROUP, 1, LANES), f32),
            jax.ShapeDtypeStruct((3, LANES), f32),
        ),
        in_specs=[VMEM] * 3,
        out_specs=(VMEM, VMEM),
        scratch_shapes=[pltpu.VMEM((3, GROUP, LANES), f32), pltpu.VMEM((BLOCK, LANES), f32)],
        compiler_params=pltpu.CompilerParams(vmem_limit_bytes=20 << 20),
        name="second_pass",
    )(got, cols, t)
    flows = everyone(partial, LINE)
    devices = GROUP * GROUP
    three = pl.pallas_call(
        advance,
        out_shape=jax.ShapeDtypeStruct((3 * devices, LANES), f32),
        in_specs=[VMEM] * 2,
        out_specs=VMEM,
        compiler_params=pltpu.CompilerParams(vmem_limit_bytes=4 << 20),
        name="advance",
    )(flows, own)
    spread = everyone(three.reshape(devices, 1, 3 * LANES), AXES)
    dist, change = pl.pallas_call(
        finish,
        out_shape=(jax.ShapeDtypeStruct((1, LANES), f32), jax.ShapeDtypeStruct((1, LANES), f32)),
        in_specs=[VMEM, VMEM],
        out_specs=(VMEM, VMEM),
        compiler_params=pltpu.CompilerParams(vmem_limit_bytes=4 << 20),
        name="finish",
    )(spread.reshape(3 * devices, LANES), three)
    return dist.reshape(LANES), change[0, :2]


def solution(mesh):
    torus = Mesh(mesh.devices.reshape(4, 4, 8, 2), AXES)
    return jax.shard_map(
        on_device,
        mesh=torus,
        in_specs=(P(None, AXES), P(AXES)),
        out_specs=(P(AXES), P()),
        check_vma=False,
    )
```

time: 355 us -> 103 us (0.29)
  matrix products: 79.7 us -> 0 us
  blocking collectives: 153 us -> 94 us
  starting transfers between devices: 39.7 us -> 0 us
  waiting for transfers between devices: 22.1 us -> 0 us
  local copies, waits for them, and re-layouts: 21.5 us -> 0.63 us
  between operations: 14.1 us -> 0.67 us
  other arithmetic: 12.9 us -> 0.85 us
  loops' own time: 10.7 us -> 0 us
  Pallas kernels: 0 us -> 6.38 us
    dot_general x32 -> x0, matrix products: 79.7 us -> none  [the longest x16 50 us: one_block(): jnp.einsum('kr,kc->rc', row_side, segment, precision=lax.Precision.HIGHEST)]
    psum x8 -> x0, blocking collectives: 79.1 us -> none  [one_axis_at_a_time(): return functools.reduce(lax.psum, axes, array)]
    all_to_all x6 -> x5, blocking collectives: 51.7 us -> 94 us  [everyone(): return lax.all_to_all(array, axes, split_axis=0, concat_axis=0, tiled=True)]
    all_to_all x6 -> x0, starting transfers between devices: 39.6 us -> none  [the longest x3 24.3 us: copy_for_each(): return lax.all_to_all(copies, axis, split_axis=0, concat_axis=0, tiled=True)]
    all_to_all x6 -> x0, waiting for transfers between devices: 22.1 us -> none  [the longest x3 9.43 us: copy_for_each(): return lax.all_to_all(copies, axis, split_axis=0, concat_axis=0, tiled=True)]
    all_gather x2 -> x0, blocking collectives: 21.8 us -> none  [all_blocks(): blocks = lax.all_gather(blocks, axes[k], axis=0, tiled=True)]
    another operation x2 -> x0, loops' own time: 10.7 us -> none  [column_pass(): lax.map(one_block, jnp.arange(count_blocks, dtype=jnp.int32))]
    dynamic_slice x16 -> x0, local copies, waits for them, and re-layouts: 9.44 us -> none  [column_pass(): lax.map(one_block, jnp.arange(count_blocks, dtype=jnp.int32))]
  transfers between devices with their start and end apart: 7 -> 0, of which waited for: 4 -> 0; matrix products, arithmetic and copies ran while one was open for 3% -> 0% of each run, Pallas kernels for 0% -> 0%
where the time goes in v1:
time: 103 us; the launch traced here: 102 us
  blocking collectives  94 us (91%)
  Pallas kernels  6.38 us (6%)
    all_to_all x5, blocking collectives, everyone(): return lax.all_to_all(array, axes, split_axis=0, concat_axis=0, tiled=True)  94 us
    pallas_call x1, Pallas kernels, on_device(): pl.pallas_call(first_pass, out_shape=(jax.ShapeDtypeStruct((GROUP, 2 * GR...  3.79 us

profile of v1, /device:TPU:1, one launch (start us, length us, event | category | flops | bytes accessed | tf_op | source)
XLA Modules:
  0.0 102.5 jit_solution(8950873162983693708)
XLA Ops:
  0.6 0.1 pad.2.clone
  0.7 0.8 maximum_maximum_fusion
  1.6 18.7 %all_to_all.25.cols_ref = f32[16,72,128]{2,1,0:T(8,128)S(1)} all-to-all(f32[16,72,128]{2,1,0:T(8,128)S(1)} %broadcast_in_dim.11), channel_id=1, replica_groups=mesh['row_0'=4,'row_1'=4,'row_2'=8,'col'=2] {'row_0','row_1'}, dimensions={0} | all-to-all | bytes 1179648 | tf_op jit(solution)/shard_map/all_to_all | solution.py:125
  20.3 29.1 %all_to_all.26.rows_ref = f32[16,72,128]{2,1,0:T(8,128)S(1)} all-to-all(f32[16,72,128]{2,1,0:T(8,128)S(1)} %broadcast_in_dim.11), channel_id=1, replica_groups=mesh['row_0'=4,'row_1'=4,'row_2'=8,'col'=2] {'row_2','col'}, dimensions={0} | all-to-all | bytes 1179648 | tf_op jit(solution)/shard_map/all_to_all | solution.py:125
  49.4 3.8 %first_pass.1 = (f32[16,32,128]{2,1,0:T(8,128)S(1)}, f32[2048,2048]{1,0:T(8,128)S(1)}) custom-call(f32[16,72,128]{2,1,0:T(8,128)S(1)} %all_to_all.26.rows_ref, f32[16,72,128]{2,1,0:T(8,128)S(1)} %all_to_all.25.cols_ref), custom_call_target="tpu_custom_call" | custom-call | tf_op jit(solution)/shard_map/first_pass/pallas_call | solution.py:134
  53.2 11.3 %all_to_all.27.got_ref = f32[16,32,128]{2,1,0:T(8,128)S(1)} all-to-all(f32[16,32,128]{2,1,0:T(8,128)S(1)} %get-tuple-element.8), channel_id=1, replica_groups=mesh['row_0'=4,'row_1'=4,'row_2'=8,'col'=2] {'row_0','row_1'}, dimensions={0} | all-to-all | bytes 524288 | tf_op jit(solution)/shard_map/all_to_all | solution.py:125
  64.4 1.8 %second_pass.1 = (f32[16,1,128]{2,1,0:T(1,128)S(1)}, f32[3,128]{1,0:T(4,128)S(1)}) custom-call(f32[16,32,128]{2,1,0:T(8,128)S(1)} %all_to_all.27.got_ref, f32[16,72,128]{2,1,0:T(8,128)S(1)} %all_to_all.25.cols_ref, f32[2048,2048]{1,0:T(8,128)S(1)} %get-tuple-element.9.t_ref), custom_call_target="tpu_custom_call" | custom-call | tf_op jit(solution)/shard_map/second_pass/pallas_call | solution.py:151
  66.3 10.7 %all_to_all.28.got_ref = f32[16,1,128]{2,1,0:T(1,128)S(1)} all-to-all(f32[16,1,128]{2,1,0:T(1,128)S(1)} %get-tuple-element.10), channel_id=1, replica_groups=mesh['row_0'=4,'row_1'=4,'row_2'=8,'col'=2] {'row_2','col'}, dimensions={0} | all-to-all | bytes 16384 | tf_op jit(solution)/shard_map/all_to_all | solution.py:125
  77.1 24.2 %all_to_all.29 = f32[256,1,384]{2,1,0:T(1,128)S(1)} all-to-all(f32[256,1,384]{2,1,0:T(1,128)S(1)} %bitcast.6), channel_id=1, replica_groups=mesh['row_0'=4,'row_1'=4,'row_2'=8,'col'=2] {'row_0','row_1','row_2','col'}, dimensions={0} | all-to-all | bytes 786432 | tf_op jit(solution)/shard_map/all_to_all | solution.py:125
  101.3 0.7 finish.1
  102.0 0.5 slice_bitcast_fusion
  (3 shorter events, 0.1 us)

commit v2 on v1

--- a/solution.py
+++ b/solution.py
@@ -18,6 +18,9 @@
 BLOCK = GROUP * LANES
 STEP = 1.0 / NPOL
 SCALE = 0.125
+XROWS = 2 * GROUP
+YROWS = GROUP + 8
+ZROWS = 2 * GROUP + 8
 
 VMEM = pl.BlockSpec(memory_space=pltpu.VMEM)
 
@@ -68,19 +71,29 @@
                 out_ref[copy, pl.ds(GROUP + 2 * jt + k, 1), :] = plain[:, lane]
 
 
-def second_pass(got_ref, cols_ref, t_ref, out_ref, own_ref, u1_ref, sums):
+def second_pass(got_ref, cols_ref, t_ref, out_ref, keep, sums):
     both = jnp.sum(got_ref[...], axis=0)
     flow, totals = both[:GROUP], both[GROUP:]
     u0 = cols_ref[:, FEATS, :]
     stay = 1.0 - STEP * totals
     u1 = STEP * flow + u0 * stay
     here = jnp.sum(u1)
-    u1_ref[0] = u1
-    u1_ref[1] = stay
-    u1_ref[2] = u0
+    start = jnp.sum(u0)
+    keep[0] = u1
+    keep[1] = stay
     p = lax.axis_index(PLANE)
-    for k in range(3):
-        own_ref[pl.ds(k, 1), :] = u1_ref[k, pl.ds(p, 1), :]
+    tail = jnp.concatenate(
+        [
+            keep[0, pl.ds(p, 1), :],
+            keep[1, pl.ds(p, 1), :],
+            jnp.full((1, LANES), here),
+            jnp.full((1, LANES), start),
+            jnp.zeros((4, LANES), jnp.float32),
+        ],
+        axis=0,
+    )
+    for copy in range(GROUP):
+        out_ref[copy, pl.ds(GROUP, 8), :] = tail
     across = [jnp.broadcast_to(u1[g : g + 1], (8, LANES)) for g in range(GROUP)]
 
     def one(n, carry):
@@ -94,29 +107,37 @@
     lax.fori_loop(0, BLOCK // 8, one, 0, unroll=8)
     for g in range(GROUP):
         turned = sums[g * LANES : (g + 1) * LANES, :].T
-        out_ref[g] = 0.5 * (here - jnp.sum(turned, axis=0, keepdims=True))
-
-
-def advance(got_ref, own_ref, out_ref):
-    flow = jnp.sum(got_ref[...], axis=0)
-    u1, stay, u0 = own_ref[0:1], own_ref[1:2], own_ref[2:3]
+        row = 0.5 * (here - jnp.sum(turned, axis=0, keepdims=True))
+        for copy in range(GROUP):
+            out_ref[copy, pl.ds(g, 1), :] = row
+
+
+def advance(got_ref, rows_ref, out_ref):
+    flow = jnp.sum(got_ref[:, :GROUP, :], axis=0)
+    u1 = got_ref[:, GROUP, :]
+    stay = got_ref[:, GROUP + 1, :]
+    n1 = jnp.sum(got_ref[:, GROUP + 2, :], axis=0, keepdims=True)
+    n0 = jnp.sum(got_ref[:, GROUP + 3, :], axis=0, keepdims=True)
     u2 = STEP * flow + u1 * stay
-    three = jnp.concatenate([u2, u1, u0], axis=0)
-    many = jnp.concatenate([three] * 8, axis=0)
-    for n in range(out_ref.shape[0] // 24):
-        out_ref[pl.ds(n * 24, 24), :] = many
-
-
-def finish(all_ref, mine_ref, dist_ref, change_ref):
-    count = all_ref.shape[0] // 3
-    u2 = all_ref[pl.ds(0, count, stride=3), :]
-    u1 = all_ref[pl.ds(1, count, stride=3), :]
-    u0 = all_ref[pl.ds(2, count, stride=3), :]
-    n2, n1, n0 = jnp.sum(u2), jnp.sum(u1), jnp.sum(u0)
-    w2, w1, w0 = u2 / n2, u1 / n1, u0 / n0
-    first = jnp.sum(jnp.abs(w1 - w0))
-    second = jnp.sum(jnp.abs(w2 - w1))
-    dist_ref[...] = NPOL * (mine_ref[0:1, :] / n2)
+    w1 = u1 / n1
+    u0 = rows_ref[:, FEATS, :]
+    change = jnp.sum(jnp.abs(w1 - u0 / n0))
+    for copy in range(GROUP):
+        out_ref[copy, 0:GROUP, :] = u2
+        out_ref[copy, GROUP : 2 * GROUP, :] = w1
+        out_ref[copy, 2 * GROUP : ZROWS, :] = jnp.full((8, LANES), change)
+
+
+def finish(all_ref, dist_ref, change_ref):
+    p = lax.axis_index(PLANE)
+    q = lax.axis_index(LINE)
+    u2 = all_ref[:, :GROUP, :]
+    w1 = all_ref[:, GROUP : 2 * GROUP, :]
+    first = jnp.sum(all_ref[:, 2 * GROUP, :], axis=0, keepdims=True)
+    n2 = jnp.sum(u2)
+    second = jnp.sum(jnp.abs(u2 / n2 - w1))
+    own = all_ref[pl.ds(p, 1), pl.ds(q, 1), :].reshape(1, LANES)
+    dist_ref[...] = NPOL * (own / n2)
     lane = lax.broadcasted_iota(jnp.int32, (1, LANES), 1)
     change_ref[...] = jnp.where(lane == 0, first, second)
 
@@ -128,13 +149,12 @@
 def on_device(features, initial):
     f32 = jnp.float32
     whole = jnp.concatenate([features, initial[None], jnp.zeros((SLOT - FEATS - 1, LANES), f32)], axis=0)
-    copies = jnp.broadcast_to(whole, (GROUP, SLOT, LANES))
-    cols = everyone(copies, PLANE)
-    rows = everyone(copies, LINE)
+    cols = everyone(jnp.broadcast_to(whole, (GROUP, SLOT, LANES)), PLANE)
+    rows = lax.all_gather(whole, LINE, axis=0)
     out, t = pl.pallas_call(
         first_pass,
         out_shape=(
-            jax.ShapeDtypeStruct((GROUP, 2 * GROUP, LANES), f32),
+            jax.ShapeDtypeStruct((GROUP, XROWS, LANES), f32),
             pltpu.VMEM((BLOCK, BLOCK), f32),
         ),
         in_specs=[VMEM] * 2,
@@ -148,37 +168,33 @@
         name="first_pass",
     )(rows, cols)
     got = everyone(out, PLANE)
-    partial, own = pl.pallas_call(
+    partial = pl.pallas_call(
         second_pass,
-        out_shape=(
-            jax.ShapeDtypeStruct((GROUP, 1, LANES), f32),
-            jax.ShapeDtypeStruct((3, LANES), f32),
-        ),
+        out_shape=jax.ShapeDtypeStruct((GROUP, YROWS, LANES), f32),
         in_specs=[VMEM] * 3,
-        out_specs=(VMEM, VMEM),
-        scratch_shapes=[pltpu.VMEM((3, GROUP, LANES), f32), pltpu.VMEM((BLOCK, LANES), f32)],
+        out_specs=VMEM,
+        scratch_shapes=[pltpu.VMEM((2, GROUP, LANES), f32), pltpu.VMEM((BLOCK, LANES), f32)],
         compiler_params=pltpu.CompilerParams(vmem_limit_bytes=20 << 20),
         name="second_pass",
     )(got, cols, t)
     flows = everyone(partial, LINE)
-    devices = GROUP * GROUP
-    three = pl.pallas_call(
+    after = pl.pallas_call(
         advance,
-        out_shape=jax.ShapeDtypeStruct((3 * devices, LANES), f32),
+        out_shape=jax.ShapeDtypeStruct((GROUP, ZROWS, LANES), f32),
         in_specs=[VMEM] * 2,
         out_specs=VMEM,
         compiler_params=pltpu.CompilerParams(vmem_limit_bytes=4 << 20),
         name="advance",
-    )(flows, own)
-    spread = everyone(three.reshape(devices, 1, 3 * LANES), AXES)
+    )(flows, rows)
+    spread = everyone(after, PLANE)
     dist, change = pl.pallas_call(
         finish,
         out_shape=(jax.ShapeDtypeStruct((1, LANES), f32), jax.ShapeDtypeStruct((1, LANES), f32)),
-        in_specs=[VMEM, VMEM],
+        in_specs=[VMEM],
         out_specs=(VMEM, VMEM),
         compiler_params=pltpu.CompilerParams(vmem_limit_bytes=4 << 20),
         name="finish",
-    )(spread.reshape(3 * devices, LANES), three)
+    )(spread)
     return dist.reshape(LANES), change[0, :2]
 
 

time: 103 us -> 81.5 us (0.79)
  blocking collectives: 94 us -> 64.1 us
  starting transfers between devices: 0 us -> 7.57 us
    all_to_all x5 -> x3, blocking collectives: 94 us -> 41.7 us  [everyone(): return lax.all_to_all(array, axes, split_axis=0, concat_axis=0, tiled=True)]
    all_gather x0 -> x1, blocking collectives: none -> 22.4 us  [on_device(): rows = lax.all_gather(whole, LINE, axis=0)]
    all_to_all x0 -> x1, starting transfers between devices: none -> 7.57 us  [everyone(): return lax.all_to_all(array, axes, split_axis=0, concat_axis=0, tiled=True)]
  transfers between devices with their start and end apart: 0 -> 1, of which waited for: 0 -> 0; matrix products, arithmetic and copies ran while one was open for 0% -> 0% of each run, Pallas kernels for 0% -> 0%
where the time goes in v2:
time: 81.5 us; the launch traced here: 81.2 us
  blocking collectives  64.1 us (79%)
  starting transfers between devices  7.57 us (9%)
  Pallas kernels  6.49 us (8%)
  local copies, waits for them, and re-layouts  1.45 us (2%)
  other arithmetic  0.85 us (1%)
    all_to_all x3, blocking collectives, everyone(): return lax.all_to_all(array, axes, split_axis=0, concat_axis=0, tiled=True)  41.7 us
    all_gather x1, blocking collectives, on_device(): rows = lax.all_gather(whole, LINE, axis=0)  22.4 us
    all_to_all x1, starting transfers between devices, everyone(): return lax.all_to_all(array, axes, split_axis=0, concat_axis=0, tiled=True)  7.57 us
    pallas_call x1, Pallas kernels, on_device(): pl.pallas_call(first_pass, out_shape=(jax.ShapeDtypeStruct((GROUP, XROWS,...  3.73 us
    pallas_call x1, Pallas kernels, on_device(): pl.pallas_call(second_pass, out_shape=jax.ShapeDtypeStruct((GROUP, YROWS,...  1.93 us
  transfers between devices with their start and end apart: 1, of which 0 were waited for; matrix products, arithmetic and copies ran while one was open for 0% of the time, Pallas kernels for 0%

profile of v2, /device:TPU:1, one launch (start us, length us, event | category | flops | bytes accessed | tf_op | source)
XLA Modules:
  0.0 81.2 jit_solution(511689406985094432)
XLA Ops:
  0.6 0.1 pad.2.clone
  0.7 0.8 %maximum_maximum_fusion = f32[72,128]{1,0:T(8,128)S(1)} fusion(f32[1,128]{1,0:T(1,128)} %bitcast.7, f32[64,128]{1,0:T(8,128)} %param.2, f32[72]{0:T(128)S(1)} %pad.2.clone), kind=kLoop, calls=%fused_computation | loop fusion | flops 18432 | bytes 70432 | tf_op jit(solution)/shard_map/concatenate | solution.py:151
  1.6 0.9 %broadcast_in_dim.11 = f32[16,72,128]{2,1,0:T(8,128)} broadcast(f32[72,128]{1,0:T(8,128)S(1)} %maximum_maximum_fusion), dimensions={1,2} | broadcast | bytes 626688 | tf_op jit(solution)/shard_map/broadcast_in_dim | solution.py:152
  2.4 7.6 %all-to-all-start = ((f32[16,72,128]{2,1,0:T(8,128)}), f32[16,72,128]{2,1,0:T(8,128)S(1)}, u32[]{:S(2)}, u32[]{:S(2)}) async-start(f32[16,72,128]{2,1,0:T(8,128)} %broadcast_in_dim.11), calls=%async_computation | async-start | bytes 1179648 | tf_op jit(solution)/shard_map/all_to_all | solution.py:146
  10.0 22.4 %all-gather = f32[1152,128]{1,0:T(8,128)S(1)} all-gather(f32[72,128]{1,0:T(8,128)S(1)} %maximum_maximum_fusion), channel_id=2, replica_groups=mesh['row_0'=4,'row_1'=4,'row_2'=8,'col'=2] {'row_2','col'}, dimensions={0}, use_global_device_ids=true | all-gather | bytes 626688 | tf_op jit(solution)/shard_map/all_gather | solution.py:153
  32.4 0.0 all-to-all-done.cols_ref
  32.4 3.7 %first_pass.1 = (f32[16,32,128]{2,1,0:T(8,128)S(1)}, f32[2048,2048]{1,0:T(8,128)S(1)}) custom-call(f32[16,72,128]{2,1,0:T(8,128)S(1)} %bitcast.5, f32[16,72,128]{2,1,0:T(8,128)S(1)} %all-to-all-done.cols_ref), custom_call_target="tpu_custom_call" | custom-call | tf_op jit(solution)/shard_map/first_pass/pallas_call | solution.py:154
  36.1 15.1 %all_to_all.20.got_ref = f32[16,32,128]{2,1,0:T(8,128)S(1)} all-to-all(f32[16,32,128]{2,1,0:T(8,128)S(1)} %get-tuple-element.6), channel_id=1, replica_groups=mesh['row_0'=4,'row_1'=4,'row_2'=8,'col'=2] {'row_0','row_1'}, dimensions={0} | all-to-all | bytes 524288 | tf_op jit(solution)/shard_map/all_to_all | solution.py:146
  51.2 1.9 %second_pass.1 = f32[16,24,128]{2,1,0:T(8,128)S(1)} custom-call(f32[16,32,128]{2,1,0:T(8,128)S(1)} %all_to_all.20.got_ref, f32[16,72,128]{2,1,0:T(8,128)S(1)} %all-to-all-done.cols_ref, f32[2048,2048]{1,0:T(8,128)S(1)} %get-tuple-element.7.t_ref), custom_call_target="tpu_custom_call" | custom-call | tf_op jit(solution)/shard_map/second_pass/pallas_call | solution.py:171
  53.1 14.9 %all_to_all.21.got_ref = f32[16,24,128]{2,1,0:T(8,128)S(1)} all-to-all(f32[16,24,128]{2,1,0:T(8,128)S(1)} %second_pass.1), channel_id=1, replica_groups=mesh['row_0'=4,'row_1'=4,'row_2'=8,'col'=2] {'row_2','col'}, dimensions={0} | all-to-all | bytes 393216 | tf_op jit(solution)/shard_map/all_to_all | solution.py:146
  68.1 0.2 advance.1
  68.2 11.7 %all_to_all.22.all_ref = f32[16,40,128]{2,1,0:T(8,128)S(1)} all-to-all(f32[16,40,128]{2,1,0:T(8,128)S(1)} %advance.1), channel_id=1, replica_groups=mesh['row_0'=4,'row_1'=4,'row_2'=8,'col'=2] {'row_0','row_1'}, dimensions={0} | all-to-all | bytes 655360 | tf_op jit(solution)/shard_map/all_to_all | solution.py:146
  80.0 0.7 finish.1
  80.7 0.5 slice_bitcast_fusion
  (1 shorter events, 0.0 us)
Async XLA Ops:
  2.4 30.0 %all-to-all-start = ((f32[16,72,128]{2,1,0:T(8,128)}), f32[16,72,128]{2,1,0:T(8,128)S(1)}, u32[]{:S(2)}, u32[]{:S(2)}) async-start(f32[16,72,128]{2,1,0:T(8,128)} %broadcast_in_dim.11), calls=%async_computation | async-start | bytes 1179648 | tf_op jit(solution)/shard_map/all_to_all | solution.py:146

commit v3 on v2

v3 whole, which is shorter than its diff:
```python
import jax
import jax.numpy as jnp
from jax import lax
from jax.experimental import pallas as pl
from jax.experimental.pallas import tpu as pltpu
from jax.sharding import Mesh
from jax.sharding import PartitionSpec as P

NPOL = 32768
AXES = ("row_0", "row_1", "row_2", "col")
PLANE = ("row_0", "row_1")
LINE = ("row_2", "col")
HALF = 32
FEATS = 64
SLOT = 72
LANES = 128
GROUP = 16
BLOCK = GROUP * LANES
STEP = 1.0 / NPOL
SCALE = 0.125
XROWS = GROUP + 1
YROWS = GROUP + 3
ZROWS = 2 * GROUP + 1

VMEM = pl.BlockSpec(memory_space=pltpu.VMEM)


def halves(x):
    high = x.astype(jnp.bfloat16).astype(jnp.float32)
    return high, x - high


def pack(features_ref, initial_ref, whole_ref, copies_ref):
    tail = jnp.concatenate([initial_ref[...], jnp.zeros((SLOT - FEATS - 1, LANES), jnp.float32)], axis=0)
    whole = jnp.concatenate([features_ref[...], tail], axis=0)
    whole_ref[...] = whole
    for copy in range(GROUP):
        copies_ref[copy] = whole


def first_pass(rows_ref, cols_ref, out_ref, t_ref, lhs, rhs, mass):
    total = jnp.zeros((1, LANES), jnp.float32)
    for g in range(GROUP):
        x = rows_ref[g]
        a, b = x[:HALF] * SCALE, x[HALF:FEATS] * SCALE
        high, low = halves(jnp.concatenate([b, -a], axis=0))
        at = pl.ds(g * LANES, LANES)
        turned = jnp.concatenate([high, low], axis=0).T.astype(jnp.bfloat16)
        lhs[at, 0:LANES] = turned
        lhs[at, LANES : 2 * LANES] = turned
        u = x[FEATS : FEATS + 1]
        total += u
        mass[at, :] = jnp.broadcast_to(u, (LANES, LANES)).T
        high, low = halves(cols_ref[g, :FEATS])
        high, low = high.astype(jnp.bfloat16), low.astype(jnp.bfloat16)
        rhs[:, at] = jnp.concatenate([high, high, low, low], axis=0)
    here = jnp.sum(total)

    width = 2 * LANES
    height = 2 * LANES
    for jt in range(BLOCK // width):
        at = pl.ds(jt * width, width)
        right = rhs[:, at]
        flow = jnp.zeros((8, width), jnp.float32)
        plain = jnp.zeros((8, width), jnp.float32)
        for ic in range(BLOCK // height):
            down = pl.ds(ic * height, height)
            t = jnp.tanh(jnp.dot(lhs[down, :], right, preferred_element_type=jnp.float32))
            t_ref[down, at] = t
            m = mass[down, :]
            weighted = t * jnp.concatenate([m, m], axis=1)
            flow += weighted.reshape(height // 8, 8, width).sum(axis=0)
            plain += t.reshape(height // 8, 8, width).sum(axis=0)
        flow = 0.5 * (here + jnp.sum(flow, axis=0, keepdims=True))
        plain = 0.5 * (BLOCK - jnp.sum(plain, axis=0, keepdims=True))
        for k in range(2):
            lane = slice(k * LANES, (k + 1) * LANES)
            block = 2 * jt + k
            gain = STEP * (flow[:, lane] - cols_ref[block, FEATS : FEATS + 1, :] * plain[:, lane])
            for copy in range(GROUP):
                out_ref[pl.ds(XROWS * copy + block, 1), :] = gain
            out_ref[pl.ds(XROWS * block + GROUP, 1), :] = plain[:, lane]


def second_pass(got_ref, cols_ref, t_ref, out_ref, keep, sums):
    u0 = cols_ref[:, FEATS, :]
    u1 = u0
    for g in range(GROUP):
        u1 += got_ref[XROWS * g : XROWS * g + GROUP, :]
    totals = jnp.sum(got_ref[pl.ds(GROUP, GROUP, stride=XROWS), :], axis=0, keepdims=True)
    here = jnp.sum(u1)
    start = jnp.sum(u0)
    keep[...] = u1
    own = keep[pl.ds(lax.axis_index(PLANE), 1), :]
    lane = lax.broadcasted_iota(jnp.int32, (1, LANES), 1)
    tail = jnp.concatenate([own, 1.0 - STEP * totals, jnp.where(lane < FEATS, here, start)], axis=0)
    for copy in range(GROUP):
        out_ref[pl.ds(YROWS * copy + GROUP, 3), :] = tail
    across = [jnp.broadcast_to(u1[g : g + 1], (8, LANES)) for g in range(GROUP)]

    def one(n, carry):
        down = pl.ds(pl.multiple_of(n * 8, 8), 8)
        acc = t_ref[down, 0:LANES] * across[0]
        for g in range(1, GROUP):
            acc += t_ref[down, g * LANES : (g + 1) * LANES] * across[g]
        sums[down, :] = acc
        return carry

    lax.fori_loop(0, BLOCK // 8, one, 0, unroll=8)
    for g in range(GROUP):
        turned = sums[g * LANES : (g + 1) * LANES, :].T
        row = 0.5 * (here - jnp.sum(turned, axis=0, keepdims=True))
        for copy in range(GROUP):
            out_ref[pl.ds(YROWS * copy + g, 1), :] = row


def advance(got_ref, rows_ref, out_ref):
    flow = got_ref[0:GROUP, :]
    for g in range(1, GROUP):
        flow += got_ref[YROWS * g : YROWS * g + GROUP, :]
    u1 = got_ref[pl.ds(GROUP, GROUP, stride=YROWS), :]
    stay = got_ref[pl.ds(GROUP + 1, GROUP, stride=YROWS), :]
    counts = jnp.sum(got_ref[pl.ds(GROUP + 2, GROUP, stride=YROWS), :], axis=0, keepdims=True)
    n1, n0 = counts[:, 0:1], counts[:, FEATS : FEATS + 1]
    u2 = STEP * flow + u1 * stay
    w1 = u1 / n1
    change = jnp.sum(jnp.abs(w1 - rows_ref[:, FEATS, :] / n0))
    last = jnp.full((1, LANES), change)
    for copy in range(GROUP):
        at = ZROWS * copy
        out_ref[at : at + GROUP, :] = u2
        out_ref[at + GROUP : at + 2 * GROUP, :] = w1
        out_ref[at + 2 * GROUP : at + ZROWS, :] = last


def finish(all_ref, dist_ref, change_ref):
    p = lax.axis_index(PLANE)
    q = lax.axis_index(LINE)
    first = jnp.sum(all_ref[pl.ds(2 * GROUP, GROUP, stride=ZROWS), :], axis=0, keepdims=True)
    u2 = [all_ref[ZROWS * g : ZROWS * g + GROUP, :] for g in range(GROUP)]
    n2 = jnp.sum(sum(u2[1:], u2[0]))
    second = jnp.zeros((GROUP, LANES), jnp.float32)
    for g in range(GROUP):
        second += jnp.abs(u2[g] / n2 - all_ref[ZROWS * g + GROUP : ZROWS * g + 2 * GROUP, :])
    dist_ref[...] = NPOL * (all_ref[pl.ds(ZROWS * p + q, 1), :] / n2)
    lane = lax.broadcasted_iota(jnp.int32, (1, 2), 1)
    change_ref[...] = jnp.where(lane == 0, first[:, 0:2], jnp.sum(second))


def everyone(array, axes):
    count, lanes = array.shape
    blocks = array.reshape(GROUP, 1, count // GROUP * lanes)
    return lax.all_to_all(blocks, axes, split_axis=0, concat_axis=0, tiled=True).reshape(count, lanes)


def call(kernel, outs, megabytes, scratch=()):
    return pl.pallas_call(
        kernel,
        out_shape=outs,
        scratch_shapes=scratch,
        compiler_params=pltpu.CompilerParams(vmem_limit_bytes=megabytes << 20),
        name=kernel.__name__,
    )


def on_device(features, initial):
    def shape(*lengths):
        return jax.ShapeDtypeStruct(lengths, jnp.float32)

    whole, copies = call(pack, (shape(SLOT, LANES), shape(GROUP, SLOT, LANES)), 62)(
        features, initial.reshape(1, LANES)
    )
    cols = lax.all_to_all(copies, PLANE, split_axis=0, concat_axis=0, tiled=True)
    rows = lax.all_gather(whole, LINE, axis=0)
    gain, t = call(
        first_pass,
        (shape(GROUP * XROWS, LANES), pltpu.VMEM((BLOCK, BLOCK), jnp.float32)),
        24,
        (
            pltpu.VMEM((BLOCK, 2 * LANES), jnp.bfloat16),
            pltpu.VMEM((2 * LANES, BLOCK), jnp.bfloat16),
            pltpu.VMEM((BLOCK, LANES), jnp.float32),
        ),
    )(rows, cols)
    flow = call(
        second_pass,
        shape(GROUP * YROWS, LANES),
        20,
        (pltpu.VMEM((GROUP, LANES), jnp.float32), pltpu.VMEM((BLOCK, LANES), jnp.float32)),
    )(everyone(gain, PLANE), cols, t)
    after = call(advance, shape(GROUP * ZROWS, LANES), 4)(everyone(flow, LINE), rows)
    dist, change = call(finish, (shape(1, LANES), shape(1, 2)), 4)(everyone(after, PLANE))
    return dist.reshape(LANES), change.reshape(2)


def solution(mesh):
    torus = Mesh(mesh.devices.reshape(4, 4, 8, 2), AXES)
    return jax.shard_map(
        on_device,
        mesh=torus,
        in_specs=(P(None, AXES), P(AXES)),
        out_specs=(P(AXES), P()),
        check_vma=False,
    )
```

time: 81.5 us -> 78.4 us (0.962)
  blocking collectives: 64.1 us -> 62 us
  local copies, waits for them, and re-layouts: 1.45 us -> 0 us
  Pallas kernels: 6.49 us -> 7.77 us
  other arithmetic: 0.85 us -> 0 us
    all_to_all x3, blocking collectives: 41.7 us -> 39.4 us  [everyone(): lax.all_to_all(blocks, axes, split_axis=0, concat_axis=0, tiled=True)]
    pallas_call x4 -> x5, Pallas kernels: 6.49 us -> 7.77 us  [the longest x1 3.21 us: on_device(): call(first_pass, (shape(GROUP * XROWS, LANES), pltpu.VMEM((BLOCK, BLOCK),...]
    broadcast_in_dim x2 -> x0, local copies, waits for them, and re-layouts: 0.86 us -> none  [the longest x1 0.86 us: on_device(): cols = everyone(jnp.broadcast_to(whole, (GROUP, SLOT, LANES)), PLANE)]
    concatenate x1 -> x0, other arithmetic: 0.85 us -> none  [on_device(): jnp.concatenate([features, initial[None], jnp.zeros((SLOT - FEATS - 1, LA...]
where the time goes in v3:
time: 78.4 us; the launch traced here: 78 us
  blocking collectives  62 us (79%)
  Pallas kernels  7.77 us (10%)
  starting transfers between devices  7.57 us (10%)
    all_to_all x3, blocking collectives, everyone(): lax.all_to_all(blocks, axes, split_axis=0, concat_axis=0, tiled=True)  39.4 us
    all_gather x1, blocking collectives, on_device(): rows = lax.all_gather(whole, LINE, axis=0)  22.6 us
    all_to_all x1, starting transfers between devices, on_device(): lax.all_to_all(copies, PLANE, split_axis=0, concat_axis=0, tiled=True)  7.57 us
    pallas_call x1, Pallas kernels, on_device(): call(first_pass, (shape(GROUP * XROWS, LANES), pltpu.VMEM((BLOCK, BLOCK),...  3.21 us
    pallas_call x1, Pallas kernels, on_device(): call(second_pass, shape(GROUP * YROWS, LANES), 20, (pltpu.VMEM((GROUP, LA...  1.93 us
    pallas_call x1, Pallas kernels, on_device(): call(pack, (shape(SLOT, LANES), shape(GROUP, SLOT, LANES)), 62)  1.64 us
  transfers between devices with their start and end apart: 1, of which 0 were waited for; matrix products, arithmetic and copies ran while one was open for 0% of the time, Pallas kernels for 0%

profile of v3, /device:TPU:1, one launch (start us, length us, event | category | flops | bytes accessed | tf_op | source)
XLA Modules:
  0.0 78.0 jit_solution(13245961707343598701)
XLA Ops:
  0.6 1.6 %pack.1 = (f32[72,128]{1,0:T(8,128)}, f32[16,72,128]{2,1,0:T(8,128)}) custom-call(f32[64,128]{1,0:T(8,128)} %features_ref.1, f32[1,128]{1,0:T(1,128)} %bitcast.18), custom_call_target="tpu_custom_call" | custom-call | tf_op jit(solution)/shard_map/pack/pallas_call | solution.py:170
  2.3 7.6 %all-to-all-start = ((f32[16,72,128]{2,1,0:T(8,128)}), f32[16,72,128]{2,1,0:T(8,128)S(1)}, u32[]{:S(2)}, u32[]{:S(2)}) async-start(f32[16,72,128]{2,1,0:T(8,128)} %get-tuple-element.9), calls=%async_computation | async-start | bytes 1179648 | tf_op jit(solution)/shard_map/all_to_all | solution.py:173
  9.8 22.6 %all-gather = f32[1152,128]{1,0:T(8,128)S(1)} all-gather(f32[72,128]{1,0:T(8,128)} %get-tuple-element.8), channel_id=2, replica_groups=mesh['row_0'=4,'row_1'=4,'row_2'=8,'col'=2] {'row_2','col'}, dimensions={0}, use_global_device_ids=true | all-gather | bytes 626688 | tf_op jit(solution)/shard_map/all_gather | solution.py:174
  32.5 0.0 all-to-all-done.cols_ref
  32.5 3.2 %first_pass.1 = (f32[272,128]{1,0:T(8,128)S(1)}, f32[2048,2048]{1,0:T(8,128)S(1)}) custom-call(f32[16,72,128]{2,1,0:T(8,128)S(1)} %bitcast.10, f32[16,72,128]{2,1,0:T(8,128)S(1)} %all-to-all-done.cols_ref), custom_call_target="tpu_custom_call" | custom-call | tf_op jit(solution)/shard_map/first_pass/pallas_call | solution.py:175
  35.7 13.6 %all_to_all.20 = f32[16,1,2176]{2,1,0:T(1,128)S(1)} all-to-all(f32[16,1,2176]{2,1,0:T(1,128)S(1)} %bitcast.17), channel_id=1, replica_groups=mesh['row_0'=4,'row_1'=4,'row_2'=8,'col'=2] {'row_0','row_1'}, dimensions={0} | all-to-all | bytes 278528 | tf_op jit(solution)/shard_map/all_to_all | solution.py:153
  49.3 1.9 %second_pass.1 = f32[304,128]{1,0:T(8,128)S(1)} custom-call(f32[272,128]{1,0:T(8,128)S(1)} %bitcast.16, f32[16,72,128]{2,1,0:T(8,128)S(1)} %all-to-all-done.cols_ref, f32[2048,2048]{1,0:T(8,128)S(1)} %get-tuple-element.11.t_ref), custom_call_target="tpu_custom_call" | custom-call | tf_op jit(solution)/shard_map/second_pass/pallas_call | solution.py:185
  51.2 14.4 %all_to_all.21 = f32[16,1,2432]{2,1,0:T(1,128)S(1)} all-to-all(f32[16,1,2432]{2,1,0:T(1,128)S(1)} %bitcast.14), channel_id=1, replica_groups=mesh['row_0'=4,'row_1'=4,'row_2'=8,'col'=2] {'row_2','col'}, dimensions={0} | all-to-all | bytes 311296 | tf_op jit(solution)/shard_map/all_to_all | solution.py:153
  65.6 0.2 advance.1
  65.9 11.4 %all_to_all.22 = f32[16,1,4224]{2,1,0:T(1,128)S(1)} all-to-all(f32[16,1,4224]{2,1,0:T(1,128)S(1)} %bitcast.13), channel_id=1, replica_groups=mesh['row_0'=4,'row_1'=4,'row_2'=8,'col'=2] {'row_0','row_1'}, dimensions={0} | all-to-all | bytes 540672 | tf_op jit(solution)/shard_map/all_to_all | solution.py:153
  77.2 0.8 %finish.1 = (f32[1,128]{1,0:T(1,128)}, f32[1,2]{1,0:T(1,128)}) custom-call(f32[528,128]{1,0:T(8,128)S(1)} %bitcast.12), custom_call_target="tpu_custom_call" | custom-call | tf_op jit(solution)/shard_map/finish/pallas_call | solution.py:192
Async XLA Ops:
  2.3 30.2 %all-to-all-start = ((f32[16,72,128]{2,1,0:T(8,128)}), f32[16,72,128]{2,1,0:T(8,128)S(1)}, u32[]{:S(2)}, u32[]{:S(2)}) async-start(f32[16,72,128]{2,1,0:T(8,128)} %get-tuple-element.9), calls=%async_computation | async-start | bytes 1179648 | tf_op jit(solution)/shard_map/all_to_all | solution.py:173

commit v4 on v3

--- a/solution.py
+++ b/solution.py
@@ -25,9 +25,10 @@
 VMEM = pl.BlockSpec(memory_space=pltpu.VMEM)
 
 
-def halves(x):
+def pieces(x):
     high = x.astype(jnp.bfloat16).astype(jnp.float32)
-    return high, x - high
+    middle = (x - high).astype(jnp.bfloat16).astype(jnp.float32)
+    return high, middle, (x - high) - middle
 
 
 def pack(features_ref, initial_ref, whole_ref, copies_ref):
@@ -43,17 +44,17 @@
     for g in range(GROUP):
         x = rows_ref[g]
         a, b = x[:HALF] * SCALE, x[HALF:FEATS] * SCALE
-        high, low = halves(jnp.concatenate([b, -a], axis=0))
+        high, middle, low = pieces(jnp.concatenate([b, -a], axis=0))
         at = pl.ds(g * LANES, LANES)
-        turned = jnp.concatenate([high, low], axis=0).T.astype(jnp.bfloat16)
+        turned = jnp.concatenate([high, middle], axis=0).T.astype(jnp.bfloat16)
         lhs[at, 0:LANES] = turned
         lhs[at, LANES : 2 * LANES] = turned
+        lhs[at, 2 * LANES : 3 * LANES] = jnp.concatenate([high, low], axis=0).T.astype(jnp.bfloat16)
         u = x[FEATS : FEATS + 1]
         total += u
         mass[at, :] = jnp.broadcast_to(u, (LANES, LANES)).T
-        high, low = halves(cols_ref[g, :FEATS])
-        high, low = high.astype(jnp.bfloat16), low.astype(jnp.bfloat16)
-        rhs[:, at] = jnp.concatenate([high, high, low, low], axis=0)
+        high, middle, low = (y.astype(jnp.bfloat16) for y in pieces(cols_ref[g, :FEATS]))
+        rhs[:, at] = jnp.concatenate([high, high, middle, middle, low, high], axis=0)
     here = jnp.sum(total)
 
     width = 2 * LANES
@@ -82,7 +83,7 @@
             out_ref[pl.ds(XROWS * block + GROUP, 1), :] = plain[:, lane]
 
 
-def second_pass(got_ref, cols_ref, t_ref, out_ref, keep, sums):
+def second_pass(got_ref, cols_ref, t_ref, out_ref, keep):
     u0 = cols_ref[:, FEATS, :]
     u1 = u0
     for g in range(GROUP):
@@ -97,18 +98,15 @@
     for copy in range(GROUP):
         out_ref[pl.ds(YROWS * copy + GROUP, 3), :] = tail
     across = [jnp.broadcast_to(u1[g : g + 1], (8, LANES)) for g in range(GROUP)]
-
-    def one(n, carry):
-        down = pl.ds(pl.multiple_of(n * 8, 8), 8)
-        acc = t_ref[down, 0:LANES] * across[0]
-        for g in range(1, GROUP):
-            acc += t_ref[down, g * LANES : (g + 1) * LANES] * across[g]
-        sums[down, :] = acc
-        return carry
-
-    lax.fori_loop(0, BLOCK // 8, one, 0, unroll=8)
-    for g in range(GROUP):
-        turned = sums[g * LANES : (g + 1) * LANES, :].T
+    for g in range(GROUP):
+        parts = []
+        for n in range(LANES // 8):
+            down = slice(g * LANES + n * 8, g * LANES + n * 8 + 8)
+            acc = t_ref[down, 0:LANES] * across[0]
+            for k in range(1, GROUP):
+                acc += t_ref[down, k * LANES : (k + 1) * LANES] * across[k]
+            parts.append(acc)
+        turned = jnp.concatenate(parts, axis=0).T
         row = 0.5 * (here - jnp.sum(turned, axis=0, keepdims=True))
         for copy in range(GROUP):
             out_ref[pl.ds(YROWS * copy + g, 1), :] = row
@@ -177,8 +175,8 @@
         (shape(GROUP * XROWS, LANES), pltpu.VMEM((BLOCK, BLOCK), jnp.float32)),
         24,
         (
-            pltpu.VMEM((BLOCK, 2 * LANES), jnp.bfloat16),
-            pltpu.VMEM((2 * LANES, BLOCK), jnp.bfloat16),
+            pltpu.VMEM((BLOCK, 3 * LANES), jnp.bfloat16),
+            pltpu.VMEM((3 * LANES, BLOCK), jnp.bfloat16),
             pltpu.VMEM((BLOCK, LANES), jnp.float32),
         ),
     )(rows, cols)
@@ -186,7 +184,7 @@
         second_pass,
         shape(GROUP * YROWS, LANES),
         20,
-        (pltpu.VMEM((GROUP, LANES), jnp.float32), pltpu.VMEM((BLOCK, LANES), jnp.float32)),
+        (pltpu.VMEM((GROUP, LANES), jnp.float32),),
     )(everyone(gain, PLANE), cols, t)
     after = call(advance, shape(GROUP * ZROWS, LANES), 4)(everyone(flow, LINE), rows)
     dist, change = call(finish, (shape(1, LANES), shape(1, 2)), 4)(everyone(after, PLANE))

time: 78.4 us -> 79.4 us (1.013)
  Pallas kernels: 7.77 us -> 8.84 us
    pallas_call x1, Pallas kernels: 3.21 us -> 4.99 us  [on_device(): call(first_pass, (shape(GROUP * XROWS, LANES), pltpu.VMEM((BLOCK, BLOCK),...]
where the time goes in v4:
time: 79.4 us; the launch traced here: 79.1 us
  blocking collectives  62 us (78%)
  Pallas kernels  8.84 us (11%)
  starting transfers between devices  7.57 us (10%)
    all_to_all x3, blocking collectives, everyone(): lax.all_to_all(blocks, axes, split_axis=0, concat_axis=0, tiled=True)  39.4 us
    all_gather x1, blocking collectives, on_device(): rows = lax.all_gather(whole, LINE, axis=0)  22.6 us
    all_to_all x1, starting transfers between devices, on_device(): lax.all_to_all(copies, PLANE, split_axis=0, concat_axis=0, tiled=True)  7.57 us
    pallas_call x1, Pallas kernels, on_device(): call(first_pass, (shape(GROUP * XROWS, LANES), pltpu.VMEM((BLOCK, BLOCK),...  4.99 us
    pallas_call x1, Pallas kernels, on_device(): call(pack, (shape(SLOT, LANES), shape(GROUP, SLOT, LANES)), 62)  1.64 us
  transfers between devices with their start and end apart: 1, of which 0 were waited for; matrix products, arithmetic and copies ran while one was open for 0% of the time, Pallas kernels for 0%

profile of v4, /device:TPU:1, one launch (start us, length us, event | category | flops | bytes accessed | tf_op | source)
XLA Modules:
  0.0 79.1 jit_solution(12393740321797688983)
XLA Ops:
  0.6 1.6 %pack.1 = (f32[72,128]{1,0:T(8,128)}, f32[16,72,128]{2,1,0:T(8,128)}) custom-call(f32[64,128]{1,0:T(8,128)} %features_ref.1, f32[1,128]{1,0:T(1,128)} %bitcast.18), custom_call_target="tpu_custom_call" | custom-call | tf_op jit(solution)/shard_map/pack/pallas_call | solution.py:168
  2.3 7.6 %all-to-all-start = ((f32[16,72,128]{2,1,0:T(8,128)}), f32[16,72,128]{2,1,0:T(8,128)S(1)}, u32[]{:S(2)}, u32[]{:S(2)}) async-start(f32[16,72,128]{2,1,0:T(8,128)} %get-tuple-element.9), calls=%async_computation | async-start | bytes 1179648 | tf_op jit(solution)/shard_map/all_to_all | solution.py:171
  9.8 22.6 %all-gather = f32[1152,128]{1,0:T(8,128)S(1)} all-gather(f32[72,128]{1,0:T(8,128)} %get-tuple-element.8), channel_id=2, replica_groups=mesh['row_0'=4,'row_1'=4,'row_2'=8,'col'=2] {'row_2','col'}, dimensions={0}, use_global_device_ids=true | all-gather | bytes 626688 | tf_op jit(solution)/shard_map/all_gather | solution.py:172
  32.5 0.0 all-to-all-done.cols_ref
  32.5 5.0 %first_pass.1 = (f32[272,128]{1,0:T(8,128)S(1)}, f32[2048,2048]{1,0:T(8,128)S(1)}) custom-call(f32[16,72,128]{2,1,0:T(8,128)S(1)} %bitcast.10, f32[16,72,128]{2,1,0:T(8,128)S(1)} %all-to-all-done.cols_ref), custom_call_target="tpu_custom_call" | custom-call | tf_op jit(solution)/shard_map/first_pass/pallas_call | solution.py:173
  37.5 13.6 %all_to_all.20 = f32[16,1,2176]{2,1,0:T(1,128)S(1)} all-to-all(f32[16,1,2176]{2,1,0:T(1,128)S(1)} %bitcast.17), channel_id=1, replica_groups=mesh['row_0'=4,'row_1'=4,'row_2'=8,'col'=2] {'row_0','row_1'}, dimensions={0} | all-to-all | bytes 278528 | tf_op jit(solution)/shard_map/all_to_all | solution.py:151
  51.1 1.2 %second_pass.1 = f32[304,128]{1,0:T(8,128)S(1)} custom-call(f32[272,128]{1,0:T(8,128)S(1)} %bitcast.16, f32[16,72,128]{2,1,0:T(8,128)S(1)} %all-to-all-done.cols_ref, f32[2048,2048]{1,0:T(8,128)S(1)} %get-tuple-element.11.t_ref), custom_call_target="tpu_custom_call" | custom-call | tf_op jit(solution)/shard_map/second_pass/pallas_call | solution.py:183
  52.3 14.4 %all_to_all.21 = f32[16,1,2432]{2,1,0:T(1,128)S(1)} all-to-all(f32[16,1,2432]{2,1,0:T(1,128)S(1)} %bitcast.14), channel_id=1, replica_groups=mesh['row_0'=4,'row_1'=4,'row_2'=8,'col'=2] {'row_2','col'}, dimensions={0} | all-to-all | bytes 311296 | tf_op jit(solution)/shard_map/all_to_all | solution.py:151
  66.7 0.2 advance.1
  66.9 11.4 %all_to_all.22 = f32[16,1,4224]{2,1,0:T(1,128)S(1)} all-to-all(f32[16,1,4224]{2,1,0:T(1,128)S(1)} %bitcast.13), channel_id=1, replica_groups=mesh['row_0'=4,'row_1'=4,'row_2'=8,'col'=2] {'row_0','row_1'}, dimensions={0} | all-to-all | bytes 540672 | tf_op jit(solution)/shard_map/all_to_all | solution.py:151
  78.3 0.8 finish.1
Async XLA Ops:
  2.3 30.2 %all-to-all-start = ((f32[16,72,128]{2,1,0:T(8,128)}), f32[16,72,128]{2,1,0:T(8,128)S(1)}, u32[]{:S(2)}, u32[]{:S(2)}) async-start(f32[16,72,128]{2,1,0:T(8,128)} %get-tuple-element.9), calls=%async_computation | async-start | bytes 1179648 | tf_op jit(solution)/shard_map/all_to_all | solution.py:171

commit v5 on v4

--- a/solution.py
+++ b/solution.py
@@ -19,7 +19,8 @@
 STEP = 1.0 / NPOL
 SCALE = 0.125
 XROWS = GROUP + 1
-YROWS = GROUP + 3
+CHIPS = GROUP // 2
+YROWS = GROUP + 5
 ZROWS = 2 * GROUP + 1
 
 VMEM = pl.BlockSpec(memory_space=pltpu.VMEM)
@@ -95,8 +96,7 @@
     own = keep[pl.ds(lax.axis_index(PLANE), 1), :]
     lane = lax.broadcasted_iota(jnp.int32, (1, LANES), 1)
     tail = jnp.concatenate([own, 1.0 - STEP * totals, jnp.where(lane < FEATS, here, start)], axis=0)
-    for copy in range(GROUP):
-        out_ref[pl.ds(YROWS * copy + GROUP, 3), :] = tail
+    out_ref[GROUP : GROUP + 3, :] = tail
     across = [jnp.broadcast_to(u1[g : g + 1], (8, LANES)) for g in range(GROUP)]
     for g in range(GROUP):
         parts = []
@@ -108,21 +108,39 @@
             parts.append(acc)
         turned = jnp.concatenate(parts, axis=0).T
         row = 0.5 * (here - jnp.sum(turned, axis=0, keepdims=True))
-        for copy in range(GROUP):
-            out_ref[pl.ds(YROWS * copy + g, 1), :] = row
+        at = g % 2 * CHIPS + g // 2
+        out_ref[at : at + 1, :] = row
+
+
+def join(mine_ref, other_ref, out_ref):
+    zero = lax.axis_index("col") == 0
+    mine, other = mine_ref[GROUP : GROUP + 3, :], other_ref[GROUP : GROUP + 3, :]
+    even, odd = jnp.where(zero, mine, other), jnp.where(zero, other, mine)
+    flow = mine_ref[0:GROUP, :] + other_ref[0:GROUP, :]
+    tail = jnp.concatenate([even[0:1], odd[0:1], even[1:2], odd[1:2], mine[2:3] + other[2:3]], axis=0)
+    for copy in range(CHIPS):
+        at = YROWS * copy
+        out_ref[at : at + GROUP, :] = flow
+        out_ref[at + GROUP : at + YROWS, :] = tail
 
 
 def advance(got_ref, rows_ref, out_ref):
+    def every(row):
+        return got_ref[pl.ds(row, CHIPS, stride=YROWS), :]
+
     flow = got_ref[0:GROUP, :]
-    for g in range(1, GROUP):
-        flow += got_ref[YROWS * g : YROWS * g + GROUP, :]
-    u1 = got_ref[pl.ds(GROUP, GROUP, stride=YROWS), :]
-    stay = got_ref[pl.ds(GROUP + 1, GROUP, stride=YROWS), :]
-    counts = jnp.sum(got_ref[pl.ds(GROUP + 2, GROUP, stride=YROWS), :], axis=0, keepdims=True)
+    for k in range(1, CHIPS):
+        flow += got_ref[YROWS * k : YROWS * k + GROUP, :]
+    u1 = jnp.concatenate([every(GROUP), every(GROUP + 1)], axis=0)
+    stay = jnp.concatenate([every(GROUP + 2), every(GROUP + 3)], axis=0)
+    counts = jnp.sum(every(GROUP + 4), axis=0, keepdims=True)
     n1, n0 = counts[:, 0:1], counts[:, FEATS : FEATS + 1]
+    u0 = jnp.concatenate(
+        [rows_ref[2 * k + c, FEATS : FEATS + 1, :] for c in range(2) for k in range(CHIPS)], axis=0
+    )
     u2 = STEP * flow + u1 * stay
     w1 = u1 / n1
-    change = jnp.sum(jnp.abs(w1 - rows_ref[:, FEATS, :] / n0))
+    change = jnp.sum(jnp.abs(w1 - u0 / n0))
     last = jnp.full((1, LANES), change)
     for copy in range(GROUP):
         at = ZROWS * copy
@@ -133,7 +151,7 @@
 
 def finish(all_ref, dist_ref, change_ref):
     p = lax.axis_index(PLANE)
-    q = lax.axis_index(LINE)
+    q = CHIPS * lax.axis_index("col") + lax.axis_index("row_2")
     first = jnp.sum(all_ref[pl.ds(2 * GROUP, GROUP, stride=ZROWS), :], axis=0, keepdims=True)
     u2 = [all_ref[ZROWS * g : ZROWS * g + GROUP, :] for g in range(GROUP)]
     n2 = jnp.sum(sum(u2[1:], u2[0]))
@@ -147,7 +165,8 @@
 
 def everyone(array, axes):
     count, lanes = array.shape
-    blocks = array.reshape(GROUP, 1, count // GROUP * lanes)
+    members = lax.axis_size(axes)
+    blocks = array.reshape(members, 1, count // members * lanes)
     return lax.all_to_all(blocks, axes, split_axis=0, concat_axis=0, tiled=True).reshape(count, lanes)
 
 
@@ -182,11 +201,13 @@
     )(rows, cols)
     flow = call(
         second_pass,
-        shape(GROUP * YROWS, LANES),
+        shape(GROUP + 3, LANES),
         20,
         (pltpu.VMEM((GROUP, LANES), jnp.float32),),
     )(everyone(gain, PLANE), cols, t)
-    after = call(advance, shape(GROUP * ZROWS, LANES), 4)(everyone(flow, LINE), rows)
+    other = lax.ppermute(flow, "col", [(0, 1), (1, 0)])
+    both = call(join, shape(CHIPS * YROWS, LANES), 4)(flow, other)
+    after = call(advance, shape(GROUP * ZROWS, LANES), 4)(everyone(both, "row_2"), rows)
     dist, change = call(finish, (shape(1, LANES), shape(1, 2)), 4)(everyone(after, PLANE))
     return dist.reshape(LANES), change.reshape(2)
 

time: 79.4 us -> 77.9 us (0.981); the launches traced: 79.1 us -> 76.6 us
  blocking collectives: 62 us -> 57.1 us
  starting transfers between devices: 7.57 us -> 9.25 us
  waiting for transfers between devices: 0.01 us -> 0.84 us
    all_to_all x3, blocking collectives: 39.4 us -> 34.4 us  [everyone(): lax.all_to_all(blocks, axes, split_axis=0, concat_axis=0, tiled=True)]
    ppermute x0 -> x1, starting transfers between devices: none -> 1.68 us  [on_device(): other = lax.ppermute(flow, 'col', [(0, 1), (1, 0)])]
    ppermute x0 -> x1, waiting for transfers between devices: none -> 0.83 us  [on_device(): other = lax.ppermute(flow, 'col', [(0, 1), (1, 0)])]
  transfers between devices with their start and end apart: 1 -> 2, of which waited for: 0 -> 1; matrix products, arithmetic and copies ran while one was open for 0% -> 0% of each run, Pallas kernels for 0% -> 0%
where the time goes in v5:
time: 77.9 us; the launch traced here: 76.6 us
  blocking collectives  57.1 us (73%)
  starting transfers between devices  9.25 us (12%)
  Pallas kernels  8.82 us (11%)
  waiting for transfers between devices  0.84 us (1%)
    all_to_all x3, blocking collectives, everyone(): lax.all_to_all(blocks, axes, split_axis=0, concat_axis=0, tiled=True)  34.4 us
    all_gather x1, blocking collectives, on_device(): rows = lax.all_gather(whole, LINE, axis=0)  22.6 us
    all_to_all x1, starting transfers between devices, on_device(): lax.all_to_all(copies, PLANE, split_axis=0, concat_axis=0, tiled=True)  7.57 us
    pallas_call x1, Pallas kernels, on_device(): call(first_pass, (shape(GROUP * XROWS, LANES), pltpu.VMEM((BLOCK, BLOCK),...  4.98 us
    ppermute x1, starting transfers between devices, on_device(): other = lax.ppermute(flow, 'col', [(0, 1), (1, 0)])  1.68 us
    pallas_call x1, Pallas kernels, on_device(): call(pack, (shape(SLOT, LANES), shape(GROUP, SLOT, LANES)), 62)  1.63 us
  transfers between devices with their start and end apart: 2, of which 1 were waited for; matrix products, arithmetic and copies ran while one was open for 0% of the time, Pallas kernels for 0%

profile of v5, /device:TPU:1, one launch (start us, length us, event | category | flops | bytes accessed | tf_op | source)
XLA Modules:
  0.0 76.6 jit_solution(17571524167459515685)
XLA Ops:
  0.6 1.6 %pack.1 = (f32[72,128]{1,0:T(8,128)}, f32[16,72,128]{2,1,0:T(8,128)}) custom-call(f32[64,128]{1,0:T(8,128)} %features_ref.1, f32[1,128]{1,0:T(1,128)} %bitcast.18), custom_call_target="tpu_custom_call" | custom-call | tf_op jit(solution)/shard_map/pack/pallas_call | solution.py:187
  2.3 7.6 %all-to-all-start = ((f32[16,72,128]{2,1,0:T(8,128)}), f32[16,72,128]{2,1,0:T(8,128)S(1)}, u32[]{:S(2)}, u32[]{:S(2)}) async-start(f32[16,72,128]{2,1,0:T(8,128)} %get-tuple-element.9), calls=%async_computation | async-start | bytes 1179648 | tf_op jit(solution)/shard_map/all_to_all | solution.py:190
  9.8 22.6 %all-gather = f32[1152,128]{1,0:T(8,128)S(1)} all-gather(f32[72,128]{1,0:T(8,128)} %get-tuple-element.8), channel_id=2, replica_groups=mesh['row_0'=4,'row_1'=4,'row_2'=8,'col'=2] {'row_2','col'}, dimensions={0}, use_global_device_ids=true | all-gather | bytes 626688 | tf_op jit(solution)/shard_map/all_gather | solution.py:191
  32.5 0.0 all-to-all-done.cols_ref
  32.5 5.0 %first_pass.1 = (f32[272,128]{1,0:T(8,128)S(1)}, f32[2048,2048]{1,0:T(8,128)S(1)}) custom-call(f32[16,72,128]{2,1,0:T(8,128)S(1)} %bitcast.10, f32[16,72,128]{2,1,0:T(8,128)S(1)} %all-to-all-done.cols_ref), custom_call_target="tpu_custom_call" | custom-call | tf_op jit(solution)/shard_map/first_pass/pallas_call | solution.py:192
  37.5 13.6 %all_to_all.20 = f32[16,1,2176]{2,1,0:T(1,128)S(1)} all-to-all(f32[16,1,2176]{2,1,0:T(1,128)S(1)} %bitcast.17), channel_id=1, replica_groups=mesh['row_0'=4,'row_1'=4,'row_2'=8,'col'=2] {'row_0','row_1'}, dimensions={0} | all-to-all | bytes 278528 | tf_op jit(solution)/shard_map/all_to_all | solution.py:170
  51.1 1.2 %second_pass.1.mine_ref = f32[19,128]{1,0:T(8,128)S(1)} custom-call(f32[272,128]{1,0:T(8,128)S(1)} %bitcast.14, f32[16,72,128]{2,1,0:T(8,128)S(1)} %all-to-all-done.cols_ref, f32[2048,2048]{1,0:T(8,128)S(1)} %get-tuple-element.11.t_ref), custom_call_target="tpu_custom_call" | custom-call | tf_op jit(solution)/shard_map/second_pass/pallas_call | solution.py:202
  52.3 1.7 %collective-permute-start = (f32[19,128]{1,0:T(8,128)S(1)}, f32[19,128]{1,0:T(8,128)S(1)}, u32[]{:S(2)}, u32[]{:S(2)}) collective-permute-start(f32[19,128]{1,0:T(8,128)S(1)} %second_pass.1.mine_ref), channel_id=1, source_target_pairs={{0,1},{1,0},{2,3},{3,2},{4,5},{5,4},{6,7},{7,6},{8,9},{9,8},{10,11... | collective-permute-start | bytes 29192 | tf_op jit(solution)/shard_map/ppermute | solution.py:208
  53.9 0.8 %collective-permute-done.other_ref = f32[19,128]{1,0:T(8,128)S(1)} collective-permute-done((f32[19,128]{1,0:T(8,128)S(1)}, f32[19,128]{1,0:T(8,128)S(1)}, u32[]{:S(2)}, u32[]{:S(2)}) %collective-permute-start) | collective-permute-done | bytes 9760 | tf_op jit(solution)/shard_map/ppermute | solution.py:208
  54.8 10.5 %all_to_all.21 = f32[8,1,2688]{2,1,0:T(1,128)S(1)} all-to-all(f32[8,1,2688]{2,1,0:T(1,128)S(1)} %bitcast.15), channel_id=1, replica_groups=mesh['row_0'=4,'row_1'=4,'row_2'=8,'col'=2] {'row_2'}, dimensions={0} | all-to-all | bytes 172032 | tf_op jit(solution)/shard_map/all_to_all | solution.py:170
  65.3 0.2 advance.1
  65.5 10.4 %all_to_all.22 = f32[16,1,4224]{2,1,0:T(1,128)S(1)} all-to-all(f32[16,1,4224]{2,1,0:T(1,128)S(1)} %bitcast.13), channel_id=1, replica_groups=mesh['row_0'=4,'row_1'=4,'row_2'=8,'col'=2] {'row_0','row_1'}, dimensions={0} | all-to-all | bytes 540672 | tf_op jit(solution)/shard_map/all_to_all | solution.py:170
  75.9 0.8 %finish.1 = (f32[1,128]{1,0:T(1,128)}, f32[1,2]{1,0:T(1,128)}) custom-call(f32[528,128]{1,0:T(8,128)S(1)} %bitcast.12), custom_call_target="tpu_custom_call" | custom-call | tf_op jit(solution)/shard_map/finish/pallas_call | solution.py:211
  (1 shorter events, 0.0 us)
Async XLA Ops:
  2.3 30.2 %all-to-all-start = ((f32[16,72,128]{2,1,0:T(8,128)}), f32[16,72,128]{2,1,0:T(8,128)S(1)}, u32[]{:S(2)}, u32[]{:S(2)}) async-start(f32[16,72,128]{2,1,0:T(8,128)} %get-tuple-element.9), calls=%async_computation | async-start | bytes 1179648 | tf_op jit(solution)/shard_map/all_to_all | solution.py:190
  52.3 2.5 %collective-permute-start = (f32[19,128]{1,0:T(8,128)S(1)}, f32[19,128]{1,0:T(8,128)S(1)}, u32[]{:S(2)}, u32[]{:S(2)}) collective-permute-start(f32[19,128]{1,0:T(8,128)S(1)} %second_pass.1.mine_ref), channel_id=1, source_target_pairs={{0,1},{1,0},{2,3},{3,2},{4,5},{5,4},{6,7},{7,6},{8,9},{9,8},{10,11... | collective-permute-start | bytes 29192 | tf_op jit(solution)/shard_map/ppermute | solution.py:208
